TPU v7x, 256 devices: a 4x2x16 block of a 4x16x16 slice. The times are simulated.
256 devices in a mesh: groups: 2 (over y), dp: 32 (over z, core), mp: 4 (over x).
Axes of the slice: x: 4, y: 2, z: 16, core: 2. Of those that a mesh axis runs over, the one named last changes fastest.
The devices are a block of a 4x16x16 slice.
Arguments:
- tokens: bfloat16 [8192, 7168], P(('groups', 'dp')), parts along dimension 0, may hold values from -20 to 20, as said below
- w_down: bfloat16 [7168, 1536], P('dp', 'mp'), may hold values from -3 to 3, as said below
- gain: float32 [1536], P('mp'), may hold values from 0.25 to 1.75
- w_up: bfloat16 [1536, 26112], P('dp', 'mp'), may hold values from -0.15625 to 0.15625
- head_counts: int32 [4], replicated, may hold values from 30 to 34, as said below
- cotangent: bfloat16 [8192, 26112], P(('groups', 'dp'), 'mp'), parts along dimension 0, may hold values from -6 to 6
Outputs:
- queries: bfloat16 [8192, 26112], P(('groups', 'dp'), 'mp'), parts along dimension 0
- grad_tokens: bfloat16 [8192, 7168], P(('groups', 'dp'), 'mp'), parts along dimension 0
There are 2 independent parts, one for each index of `groups`. A program takes and returns all parts, laid end to end along the dimension named above; an argument that names none is the same for every part. Nothing has to cross between parts.
Inputs may be any that keep to these rules, and one draw needn't show every extreme that they name: `tokens`: hidden states of order one with token scales that differ. `w_down`: entries of order 7168^(-1/2). `head_counts`: the entries sum to 128; one of them is 34.
All inputs are finite; a program needn't handle non-finite values.
Results may differ from a plain program's by a relative error of at most 0.018.
Values may be sent and summed in bfloat16 or wider, within the bound.
A program may use at most 128 MiB of HBM per device.

v0:
```python
import jax
import jax.numpy as jnp
from jax import lax
from jax.sharding import PartitionSpec as P

HD = 192


def laid_out(blocks, dim):
    shape = list(blocks.shape[1:])
    shape[dim] *= blocks.shape[0]
    return jnp.moveaxis(blocks, 0, dim).reshape(shape)


def from_everyone(array, axis):
    size = lax.axis_size(axis)
    return lax.all_to_all(
        jnp.broadcast_to(array[None], (size, *array.shape)), axis, 0, 0, tiled=True
    )


def gather_directly(array, axis, dim):
    return laid_out(from_everyone(array, axis), dim)


def cut_along(array, dim, size):
    shape = array.shape
    blocks = array.reshape(*shape[:dim], size, shape[dim] // size, *shape[dim + 1 :])
    return jnp.moveaxis(blocks, dim, 0)


def sent_and_summed(array, axis, dim):
    size = lax.axis_size(axis)
    blocks = lax.all_to_all(cut_along(array, dim, size), axis, 0, 0, tiled=True)
    return jnp.sum(blocks.astype(jnp.float32), axis=0)


def contract_last(left, right):
    return lax.dot_general(
        left, right, (((1,), (1,)), ((), ())), preferred_element_type=jnp.float32
    )


def body(tokens, w_down, gain, w_up, head_counts, cotangent):
    block_cols = w_up.shape[1]
    latent_width = w_down.shape[1] * lax.axis_size("mp")
    position = lax.axis_index("mp")
    held_heads = lax.dynamic_slice_in_dim(head_counts, position, 1, 0)
    slot_index = jnp.arange(block_cols, dtype=jnp.int32) // HD
    keep_mask = (slot_index < held_heads).astype(jnp.float32)
    down_whole = lax.all_gather(w_down, "dp", axis=0, tiled=True)
    latent_raw = jnp.dot(tokens, down_whole, preferred_element_type=jnp.float32)
    squares = lax.psum(jnp.sum(latent_raw * latent_raw, axis=1, keepdims=True), "mp")
    root_mean = jnp.sqrt(squares / latent_width + 1e-06)
    latent_local = (latent_raw / root_mean * gain).astype(jnp.bfloat16)
    latent = gather_directly(latent_local, "mp", 1)
    masked = cotangent * keep_mask.astype(jnp.bfloat16)
    up_whole = lax.all_gather(w_up, "dp", axis=0, tiled=True)
    query_total = jnp.dot(latent, up_whole, preferred_element_type=jnp.float32)
    grad_partial = contract_last(masked, up_whole)
    queries = (query_total * keep_mask).astype(jnp.bfloat16)
    grad_latent = sent_and_summed(grad_partial.astype(jnp.bfloat16), "mp", 1)
    inner_dot = lax.psum(jnp.sum(gain * grad_latent * latent_raw, axis=1, keepdims=True), "mp")
    grad_raw = (
        gain * grad_latent / root_mean - latent_raw * inner_dot / (latent_width * root_mean**3)
    ).astype(jnp.bfloat16)
    partial_value = contract_last(grad_raw, down_whole).astype(jnp.bfloat16).astype(jnp.float32)
    grad_tokens = sent_and_summed(partial_value.astype(jnp.bfloat16), "mp", 1).astype(jnp.bfloat16)
    return (queries, grad_tokens)


def solution(mesh):
    in_specs = (
        P(("groups", "dp"), None),
        P("dp", "mp"),
        P("mp"),
        P("dp", "mp"),
        P(),
        P(("groups", "dp"), "mp"),
    )
    out_specs = (P(("groups", "dp"), "mp"), P(("groups", "dp"), "mp"))
    return jax.shard_map(body, mesh=mesh, in_specs=in_specs, out_specs=out_specs, check_vma=False)
```

profile of v0, /device:TPU:40, one launch (start us, length us, event | category | flops | bytes accessed | tf_op | source)
XLA Modules:
  0.0 279.0 jit_solution(305809374449515332)
XLA Ops:
  7.2 0.0 copy-start
  7.2 0.1 all-gather.5.cloned.1.call-start
  7.3 0.7 all-gather.5.cloned.1.call-update
  8.0 0.1 all-gather.3.cloned.1.call-start
  8.1 0.7 all-gather.3.cloned.1.call-update
  8.8 1.2 dynamic_slice.3
  10.0 0.7 fusion.12
  10.7 0.0 copy-start.1
  10.7 133.8 %all-gather.5.cloned.1.call-done = bf16[1536,6528]{1,0:T(8,128)(2,1)} async-done(((bf16[48,6528]{1,0:T(8,128)(2,1)}), bf16[1536,6528]{1,0:T(8,128)(2,1)}) %all-gather.5.cloned.1.call-update) | async-done | bytes 20054032 | tf_op jit(solution)/shard_map/all_gather | solution.py:58
  144.5 10.2 %convolution_convert_fusion.1 = bf16[128,1536]{1,0:T(8,128)(2,1)S(1)} fusion(bf16[1536,6528]{1,0:T(8,128)(2,1)} %all-gather.5.cloned.1.call-done, bf16[128,6528]{1,0:T(8,128)(2,1)} %param.11, bf16[6528]{0:T(1024)(128)(2,1)S(1)} %fusion.12), kind=kOutput, calls=%fused_computation.3 | convolution fusion | flops 2567946240 | bytes 22131456 | tf_op jit(solution)/shard_map/dot_general | solution.py:39
  154.7 12.5 %all_to_all.15 = bf16[4,128,384]{2,1,0:T(8,128)(2,1)S(1)} all-to-all(bf16[4,128,384]{2,1,0:T(8,128)(2,1)S(1)} %bitcast.33), channel_id=1, replica_groups=mesh['groups'=2,'dp'=32,'mp'=4] {'mp'}, dimensions={0} | all-to-all | bytes 786432 | tf_op jit(solution)/shard_map/all_to_all | solution.py:34
  167.3 50.5 %all-gather.3.cloned.1.call-done = bf16[7168,384]{1,0:T(8,128)(2,1)} async-done(((bf16[224,384]{1,0:T(8,128)(2,1)}), bf16[7168,384]{1,0:T(8,128)(2,1)}) %all-gather.3.cloned.1.call-update) | async-done | bytes 5505040 | tf_op jit(solution)/shard_map/all_gather | solution.py:51
  217.8 0.0 copy-done
  217.8 0.0 copy-done.1
  217.9 3.8 %multiply_reduce_fusion = (f32[128]{0:T(128)S(1)}, f32[128]{0:T(128)S(1)}, f32[128,384]{1,0:T(8,128)S(1)}) fusion(f32[128,384]{1,0:T(8,128)S(1)} %convert_reduce_fusion, f32[384]{0:T(512)S(1)} %copy-done.1, bf16[128,7168]{1,0:T(8,128)(2,1)S(1)} %copy-done, bf16[7168,384]{1,0:T(8,128)(2,1)} %all-gather.3.cloned.1.call-done), kind=kOutput, calls=%fused_computation.10 | convolution fusion | flops 704888576 | bytes 7735808 | tf_op jit(solution)/shard_map/dot_general | solution.py:52
  221.6 10.5 %all-reduce = (f32[128,1]{0,1:T(1,128)S(1)}, f32[128]{0:T(128)S(1)}) all-reduce(f32[128,1]{0,1:T(1,128)S(1)} %bitcast.34, f32[128]{0:T(128)S(1)} %get-tuple-element.2), channel_id=1, replica_groups=mesh['groups'=2,'dp'=32,'mp'=4] {'mp'}, use_global_device_ids=true, to_apply=%region_1.2 | all-reduce | flops 256 | bytes 2048 | tf_op jit(solution)/shard_map/psum | solution.py:53
  232.1 0.1 multiply_convert_fusion
  232.2 0.1 copy.9
  232.3 0.8 broadcast_in_dim.7
  233.1 3.6 %all-to-all-start = ((bf16[4,128,384]{1,2,0:T(8,128)(2,1)}), bf16[4,128,384]{1,2,0:T(8,128)(2,1)S(1)}, u32[]{:S(2)}, u32[]{:S(2)}) async-start(bf16[4,128,384]{1,2,0:T(8,128)(2,1)} %broadcast_in_dim.7), calls=%async_computation | async-start | bytes 786432 | tf_op jit(solution)/shard_map/all_to_all | solution.py:17
  236.7 4.4 %convolution_convert_fusion = bf16[128,7168]{1,0:T(8,128)(2,1)S(1)} fusion(bf16[7168,384]{1,0:T(8,128)(2,1)} %all-gather.3.cloned.1.call-done, f32[128,384]{1,0:T(8,128)S(1)} %get-tuple-element.8, f32[128,384]{1,0:T(8,128)S(1)} %convert_reduce_fusion, f32[128]{0:T(128)S(1)} %get-tuple-element.6, f32[128]{0:T(128)S(1)} %get-tuple-element.5, ...), kind=kOutput, calls=%fused_computation.2 | convolution fusion | flops 705855488 | bytes 7736320 | tf_op jit(solution)/shard_map/dot_general | solution.py:39
  241.1 1.4 copy.16
  242.5 1.5 all-to-all-done
  244.0 4.5 %all-to-all-start.2 = ((bf16[4,128,1792]{2,1,0:T(8,128)(2,1)}), bf16[4,128,1792]{2,1,0:T(8,128)(2,1)}, u32[]{:S(2)}, u32[]{:S(2)}) async-start(bf16[4,128,1792]{2,1,0:T(8,128)(2,1)} %bitcast.29), calls=%async_computation.2 | async-start | bytes 3670016 | tf_op jit(solution)/shard_map/all_to_all | solution.py:34
  248.5 0.7 fusion.10
  249.1 10.9 %fusion = bf16[128,6528]{1,0:T(8,128)(2,1)} fusion(bf16[128,1536]{0,1:T(8,128)(2,1)S(1)} %bitcast.31, bf16[1536,6528]{1,0:T(8,128)(2,1)} %all-gather.5.cloned.1.call-done, f32[6528]{0:T(1024)S(1)} %fusion.10), kind=kOutput, calls=%fused_computation.1 | convolution fusion | flops 2568585216 | bytes 22144512 | tf_op jit(solution)/shard_map/dot_general | solution.py:59
  260.0 9.5 %all-to-all-done.2 = bf16[4,128,1792]{2,1,0:T(8,128)(2,1)} async-done(((bf16[4,128,1792]{2,1,0:T(8,128)(2,1)}), bf16[4,128,1792]{2,1,0:T(8,128)(2,1)}, u32[]{:S(2)}, u32[]{:S(2)}) %all-to-all-start.2) | async-done | bytes 1835040 | tf_op jit(solution)/shard_map/all_to_all | solution.py:34
  269.5 2.7 reduce_sum.42
  (3 shorter events, 0.1 us)
Async XLA Ops:
  7.2 210.7 %copy-start = (bf16[128,7168]{1,0:T(8,128)(2,1)S(1)}, bf16[128,7168]{1,0:T(8,128)(2,1)}, u32[]{:S(2)}) copy-start(bf16[128,7168]{1,0:T(8,128)(2,1)} %param.6) | copy-start | bytes 5505028
  7.2 137.3 %all-gather.5.cloned.1.call-start = ((), (), s32[]{:S(2)}) async-start(), calls=%async_computation.4 | async-start | bytes 20680704 | tf_op jit(solution)/shard_map/all_gather | solution.py:58
  8.0 209.9 %all-gather.3.cloned.1.call-start = ((), (), s32[]{:S(2)}) async-start(), calls=%async_computation.3 | async-start | bytes 5677056 | tf_op jit(solution)/shard_map/all_gather | solution.py:51
  10.7 207.1 %copy-start.1 = (f32[384]{0:T(512)S(1)}, f32[384]{0:T(512)}, u32[]{:S(2)}) copy-start(f32[384]{0:T(512)} %param.8) | copy-start | bytes 4612
  233.1 10.8 %all-to-all-start = ((bf16[4,128,384]{1,2,0:T(8,128)(2,1)}), bf16[4,128,384]{1,2,0:T(8,128)(2,1)S(1)}, u32[]{:S(2)}, u32[]{:S(2)}) async-start(bf16[4,128,384]{1,2,0:T(8,128)(2,1)} %broadcast_in_dim.7), calls=%async_computation | async-start | bytes 786432 | tf_op jit(solution)/shard_map/all_to_all | solution.py:17
  244.0 25.5 %all-to-all-start.2 = ((bf16[4,128,1792]{2,1,0:T(8,128)(2,1)}), bf16[4,128,1792]{2,1,0:T(8,128)(2,1)}, u32[]{:S(2)}, u32[]{:S(2)}) async-start(bf16[4,128,1792]{2,1,0:T(8,128)(2,1)} %bitcast.29), calls=%async_computation.2 | async-start | bytes 3670016 | tf_op jit(solution)/shard_map/all_to_all | solution.py:34
Sparse Core Ops, SparseCore 0:
  9.9 134.5 all-gather.4
  146.3 71.4 all-gather.2
where the time goes:
time: 279 us
  waiting for transfers between devices  197 us (71%)
  matrix products  29.2 us (10%)
  blocking collectives  23 us (8%)
  between operations  14.2 us (5%)
  starting transfers between devices  8.15 us (3%)
  other arithmetic  4.13 us (1%)
  local copies, waits for them, and re-layouts  3.65 us (1%)
    all_gather x1, waiting for transfers between devices, body(): up_whole = lax.all_gather(w_up, 'dp', axis=0, tiled=True)  134 us
    all_gather x1, waiting for transfers between devices, body(): down_whole = lax.all_gather(w_down, 'dp', axis=0, tiled=True)  50.5 us
    dot_general x2, matrix products, contract_last(): lax.dot_general(left, right, (((1,), (1,)), ((), ())), preferred_element_...  14.6 us
    all_to_all x1, blocking collectives, sent_and_summed(): blocks = lax.all_to_all(cut_along(array, dim, size), axis, 0, 0, tiled=True)  12.5 us
    dot_general x1, matrix products, body(): query_total = jnp.dot(latent, up_whole, preferred_element_type=jnp.float32)  10.9 us
    psum x1, blocking collectives, body(): lax.psum(jnp.sum(latent_raw * latent_raw, axis=1, keepdims=True), 'mp')  10.5 us
    all_to_all x1, waiting for transfers between devices, sent_and_summed(): blocks = lax.all_to_all(cut_along(array, dim, size), axis, 0, 0, tiled=True)  9.51 us
  transfers between devices with their start and end apart: 4, of which 4 were waited for; matrix products, arithmetic and copies ran while one was open for 11% of the time, Pallas kernels for 0%

commit v1 on v0

--- a/solution.py
+++ b/solution.py
@@ -48,7 +48,9 @@
     held_heads = lax.dynamic_slice_in_dim(head_counts, position, 1, 0)
     slot_index = jnp.arange(block_cols, dtype=jnp.int32) // HD
     keep_mask = (slot_index < held_heads).astype(jnp.float32)
-    down_whole = lax.all_gather(w_down, "dp", axis=0, tiled=True)
+    down_whole = jnp.concatenate(
+        lax.all_to_all(jnp.stack([w_down] * lax.axis_size("dp")), "dp", 0, 0), axis=0
+    )
     latent_raw = jnp.dot(tokens, down_whole, preferred_element_type=jnp.float32)
     squares = lax.psum(jnp.sum(latent_raw * latent_raw, axis=1, keepdims=True), "mp")
     root_mean = jnp.sqrt(squares / latent_width + 1e-06)

time: 279 us -> 485 us (1.74)
  waiting for transfers between devices: 197 us -> 388 us
  starting transfers between devices: 8.15 us -> 18.2 us
    all_to_all x0 -> x1, waiting for transfers between devices: none -> 242 us  [body(): lax.all_to_all(jnp.stack([w_down] * lax.axis_size('dp')), 'dp', 0, 0)]
    all_gather x1 -> x0, waiting for transfers between devices: 50.5 us -> none  [body(): down_whole = lax.all_gather(w_down, 'dp', axis=0, tiled=True)]
    all_to_all x0 -> x1, starting transfers between devices: none -> 10.1 us  [body(): lax.all_to_all(jnp.stack([w_down] * lax.axis_size('dp')), 'dp', 0, 0)]
  transfers between devices with their start and end apart: 4 -> 4, of which waited for: 4 -> 4; matrix products, arithmetic and copies ran while one was open for 11% -> 4% of each run, Pallas kernels for 0% -> 0%
where the time goes in v1:
time: 485 us; the launch traced here: 482 us
  waiting for transfers between devices  388 us (80%)
  matrix products  29.2 us (6%)
  blocking collectives  21.5 us (4%)
  starting transfers between devices  18.2 us (4%)
  between operations  14.2 us (3%)
  local copies, waits for them, and re-layouts  6.59 us (1%)
    all_to_all x1, waiting for transfers between devices, body(): lax.all_to_all(jnp.stack([w_down] * lax.axis_size('dp')), 'dp', 0, 0)  242 us
    all_gather x1, waiting for transfers between devices, body(): up_whole = lax.all_gather(w_up, 'dp', axis=0, tiled=True)  135 us
    dot_general x2, matrix products, contract_last(): lax.dot_general(left, right, (((1,), (1,)), ((), ())), preferred_element_...  14.6 us
    all_to_all x1, blocking collectives, sent_and_summed(): blocks = lax.all_to_all(cut_along(array, dim, size), axis, 0, 0, tiled=True)  12.5 us
    dot_general x1, matrix products, body(): query_total = jnp.dot(latent, up_whole, preferred_element_type=jnp.float32)  10.9 us
    all_to_all x1, starting transfers between devices, body(): lax.all_to_all(jnp.stack([w_down] * lax.axis_size('dp')), 'dp', 0, 0)  10.1 us
  transfers between devices with their start and end apart: 4, of which 4 were waited for; matrix products, arithmetic and copies ran while one was open for 4% of the time, Pallas kernels for 0%

profile of v1, /device:TPU:40, one launch (start us, length us, event | category | flops | bytes accessed | tf_op | source)
XLA Modules:
  0.0 481.7 jit_solution(10771382895924154025)
XLA Ops:
  7.2 0.0 copy-start
  7.2 0.1 all-gather.2.cloned.1.call-start
  7.3 0.7 all-gather.2.cloned.1.call-update
  8.0 1.2 dynamic_slice.3
  9.2 0.7 fusion.12
  9.9 0.0 copy-start.1
  9.9 134.6 %all-gather.2.cloned.1.call-done = bf16[1536,6528]{1,0:T(8,128)(2,1)} async-done(((bf16[48,6528]{1,0:T(8,128)(2,1)}), bf16[1536,6528]{1,0:T(8,128)(2,1)}) %all-gather.2.cloned.1.call-update) | async-done | bytes 20054032 | tf_op jit(solution)/shard_map/all_gather | solution.py:60
  144.5 10.2 %convolution_convert_fusion.1 = bf16[128,1536]{1,0:T(8,128)(2,1)S(1)} fusion(bf16[1536,6528]{1,0:T(8,128)(2,1)} %all-gather.2.cloned.1.call-done, bf16[128,6528]{1,0:T(8,128)(2,1)} %param.11, bf16[6528]{0:T(1024)(128)(2,1)S(1)} %fusion.12), kind=kOutput, calls=%fused_computation.3 | convolution fusion | flops 2567946240 | bytes 22131456 | tf_op jit(solution)/shard_map/dot_general | solution.py:39
  154.7 12.5 %all_to_all.20 = bf16[4,128,384]{2,1,0:T(8,128)(2,1)S(1)} all-to-all(bf16[4,128,384]{2,1,0:T(8,128)(2,1)S(1)} %bitcast.34), channel_id=1, replica_groups=mesh['groups'=2,'dp'=32,'mp'=4] {'mp'}, dimensions={0} | all-to-all | bytes 786432 | tf_op jit(solution)/shard_map/all_to_all | solution.py:34
  167.3 0.0 copy-done.1
  167.3 2.9 stack.2
  170.2 0.0 copy-start.2
  170.2 10.1 %all-to-all-start = ((bf16[32,224,384]{2,1,0:T(8,128)(2,1)}), bf16[32,224,384]{2,1,0:T(8,128)(2,1)}, u32[]{:S(2)}, u32[]{:S(2)}) async-start(bf16[32,224,384]{2,1,0:T(8,128)(2,1)} %stack.2), calls=%async_computation | async-start | bytes 11010048 | tf_op jit(solution)/shard_map/all_to_all | solution.py:52
  180.4 241.9 %all-to-all-done = bf16[32,224,384]{2,1,0:T(8,128)(2,1)} async-done(((bf16[32,224,384]{2,1,0:T(8,128)(2,1)}), bf16[32,224,384]{2,1,0:T(8,128)(2,1)}, u32[]{:S(2)}, u32[]{:S(2)}) %all-to-all-start) | async-done | bytes 5505056 | tf_op jit(solution)/shard_map/all_to_all | solution.py:52
  422.3 0.0 copy-done
  422.3 0.0 copy-done.2
  422.3 3.8 multiply_reduce_fusion
  426.0 8.9 %all-reduce = (f32[128,1]{0,1:T(1,128)S(1)}, f32[128]{0:T(128)S(1)}) all-reduce(f32[128,1]{0,1:T(1,128)S(1)} %bitcast.35, f32[128]{0:T(128)S(1)} %get-tuple-element.2), channel_id=1, replica_groups=mesh['groups'=2,'dp'=32,'mp'=4] {'mp'}, use_global_device_ids=true, to_apply=%region_1.2 | all-reduce | flops 256 | bytes 2048 | tf_op jit(solution)/shard_map/psum | solution.py:55
  435.0 0.1 multiply_convert_fusion
  435.1 0.1 copy.9
  435.2 0.8 broadcast_in_dim.7
  436.0 3.6 all-to-all-start.1
  439.6 4.4 convolution_convert_fusion
  444.0 1.4 copy.16
  445.4 1.5 all-to-all-done.1
  446.9 4.5 all-to-all-start.3
  451.4 0.7 fusion.10
  452.0 10.9 %fusion = bf16[128,6528]{1,0:T(8,128)(2,1)} fusion(bf16[128,1536]{0,1:T(8,128)(2,1)S(1)} %bitcast.32, bf16[1536,6528]{1,0:T(8,128)(2,1)} %all-gather.2.cloned.1.call-done, f32[6528]{0:T(1024)S(1)} %fusion.10), kind=kOutput, calls=%fused_computation.1 | convolution fusion | flops 2568585216 | bytes 22144512 | tf_op jit(solution)/shard_map/dot_general | solution.py:61
  462.9 9.3 %all-to-all-done.3 = bf16[4,128,1792]{2,1,0:T(8,128)(2,1)} async-done(((bf16[4,128,1792]{2,1,0:T(8,128)(2,1)}), bf16[4,128,1792]{2,1,0:T(8,128)(2,1)}, u32[]{:S(2)}, u32[]{:S(2)}) %all-to-all-start.3) | async-done | bytes 1835040 | tf_op jit(solution)/shard_map/all_to_all | solution.py:34
  472.2 2.7 reduce_sum.42
  (3 shorter events, 0.1 us)
Async XLA Ops:
  7.2 415.1 %copy-start = (bf16[128,7168]{1,0:T(8,128)(2,1)S(1)}, bf16[128,7168]{1,0:T(8,128)(2,1)}, u32[]{:S(2)}) copy-start(bf16[128,7168]{1,0:T(8,128)(2,1)} %param.6) | copy-start | bytes 5505028
  7.2 137.3 %all-gather.2.cloned.1.call-start = ((), (), s32[]{:S(2)}) async-start(), calls=%async_computation.4 | async-start | bytes 20680704 | tf_op jit(solution)/shard_map/all_gather | solution.py:60
  9.9 157.4 %copy-start.1 = (bf16[224,384]{1,0:T(8,128)(2,1)S(1)}, bf16[224,384]{1,0:T(8,128)(2,1)}, u32[]{:S(2)}) copy-start(bf16[224,384]{1,0:T(8,128)(2,1)} %param.7) | copy-start | bytes 516100
  170.2 252.0 %copy-start.2 = (f32[384]{0:T(512)S(1)}, f32[384]{0:T(512)}, u32[]{:S(2)}) copy-start(f32[384]{0:T(512)} %param.8) | copy-start | bytes 4612
  170.2 252.0 %all-to-all-start = ((bf16[32,224,384]{2,1,0:T(8,128)(2,1)}), bf16[32,224,384]{2,1,0:T(8,128)(2,1)}, u32[]{:S(2)}, u32[]{:S(2)}) async-start(bf16[32,224,384]{2,1,0:T(8,128)(2,1)} %stack.2), calls=%async_computation | async-start | bytes 11010048 | tf_op jit(solution)/shard_map/all_to_all | solution.py:52
  436.0 10.8 %all-to-all-start.1 = ((bf16[4,128,384]{1,2,0:T(8,128)(2,1)}), bf16[4,128,384]{1,2,0:T(8,128)(2,1)S(1)}, u32[]{:S(2)}, u32[]{:S(2)}) async-start(bf16[4,128,384]{1,2,0:T(8,128)(2,1)} %broadcast_in_dim.7), calls=%async_computation.1 | async-start | bytes 786432 | tf_op jit(solution)/shard_map/all_to_all | solution.py:17
  446.9 25.3 %all-to-all-start.3 = ((bf16[4,128,1792]{2,1,0:T(8,128)(2,1)}), bf16[4,128,1792]{2,1,0:T(8,128)(2,1)}, u32[]{:S(2)}, u32[]{:S(2)}) async-start(bf16[4,128,1792]{2,1,0:T(8,128)(2,1)} %bitcast.30), calls=%async_computation.3 | async-start | bytes 3670016 | tf_op jit(solution)/shard_map/all_to_all | solution.py:34
Sparse Core Ops, SparseCore 0:
  9.9 134.5 all-gather.1
